TPU v7x, 32 devices: a whole 2x2x4 slice. The times are simulated.
32 devices in a mesh: fsdp: 4 (over y, x), seq: 8 (over z, core).
Axes of the slice: x: 2, y: 2, z: 4, core: 2. Of those that a mesh axis runs over, the one named last changes fastest.
Arguments:
- image_input: bfloat16 [4, 1024, 1536], P('fsdp', 'seq'), may hold values from -6 to 6
- text_input: bfloat16 [4, 128, 1536], P('fsdp'), may hold values from -6 to 6
- w_qkv: bfloat16 [1536, 3, 2048], P('fsdp'), may hold values from -0.15625 to 0.15625
- query_gain: float32 [128], replicated, may hold values from 1.2 to 2.4
- key_gain: float32 [128], replicated, may hold values from 1.2 to 2.4
- image_cotangent: bfloat16 [4, 1024, 2048], P('fsdp', 'seq'), may hold values from -6 to 6
- text_cotangent: bfloat16 [4, 128, 2048], P('fsdp'), may hold values from -6 to 6
Outputs:
- image_grad: bfloat16 [4, 1024, 1536], P('fsdp', 'seq')
- text_grad: bfloat16 [4, 128, 1536], P('fsdp')
- weight_grad: float32 [1536, 3, 2048], P('fsdp', None, 'seq')
- gain_grad: float32 [2, 128], replicated
All inputs are finite; a program needn't handle non-finite values.
Results may differ from a plain program's by a relative error of at most 0.018.
The roundings to bfloat16 on the way count: a program that leaves them out, or rounds other values in their place, can miss the bound.
Values may be sent and summed in bfloat16 or wider, within the bound.
A program may use at most 192 MiB of HBM per device.

v0:
```python
import math
import jax
import jax.numpy as jnp
from jax import lax
from jax.sharding import PartitionSpec as P

HEADS = 16
HEAD = 128
epsilon = 1e-06
query_parts = 4


def rms_forward(values, gain):
    floated = values.astype(jnp.float32)
    inverse = lax.rsqrt(jnp.mean(floated * floated, axis=-1, keepdims=True) + epsilon)
    return (floated, inverse, (floated * inverse * gain).astype(jnp.bfloat16))


def rms_backward(floated, inverse, gain, incoming):
    weighted = incoming * gain
    inner_mean = jnp.mean(weighted * floated, axis=-1, keepdims=True)
    grad_input = inverse * weighted - floated * inverse * inverse * inverse * inner_mean
    grad_gain = jnp.sum(incoming * floated * inverse, axis=0)
    return (grad_input, grad_gain)


def head_backward(query_rows, key_rows, value_rows, incoming, query_gain, key_gain):
    query_float, query_inverse, query_normed = rms_forward(query_rows, query_gain)
    key_float, key_inverse, key_normed = rms_forward(key_rows, key_gain)
    length = query_rows.shape[0]
    width = query_rows.shape[1]
    block_rows = length // query_parts
    factor = 1.0 / math.sqrt(width)
    query_blocks = query_normed.reshape(query_parts, block_rows, width)
    incoming_blocks = incoming.reshape(query_parts, block_rows, width)

    def visit(carried, pieces):
        key_total, value_total = carried
        query_piece, incoming_piece = pieces
        scores = jnp.dot(query_piece, key_normed.T, preferred_element_type=jnp.float32) * factor
        attention = jax.nn.softmax(scores, axis=-1)
        attention_grad = jnp.dot(incoming_piece, value_rows.T, preferred_element_type=jnp.float32)
        row_dot = jnp.sum(attention * attention_grad, axis=-1, keepdims=True)
        score_grad = (attention * (attention_grad - row_dot)).astype(jnp.bfloat16)
        value_total = value_total + jnp.dot(
            attention.astype(jnp.bfloat16).T, incoming_piece, preferred_element_type=jnp.float32
        )
        key_total = (
            key_total
            + jnp.dot(score_grad.T, query_piece, preferred_element_type=jnp.float32) * factor
        )
        query_grad = jnp.dot(score_grad, key_normed, preferred_element_type=jnp.float32) * factor
        return ((key_total, value_total), query_grad)

    zeros_init = jnp.zeros((length, width), jnp.float32)
    (key_total, value_total), query_pieces = lax.scan(
        visit, (zeros_init, zeros_init), (query_blocks, incoming_blocks)
    )
    query_grad = query_pieces.reshape(length, width)
    query_input_grad, query_gain_grad = rms_backward(
        query_float, query_inverse, query_gain, query_grad
    )
    key_input_grad, key_gain_grad = rms_backward(key_float, key_inverse, key_gain, key_total)
    stacked = jnp.stack([query_input_grad, key_input_grad, value_total], axis=1).astype(
        jnp.bfloat16
    )
    return (stacked, jnp.stack([query_gain_grad, key_gain_grad], axis=0))


def local(image_input, text_input, w_qkv, query_gain, key_gain, image_cotangent, text_cotangent):
    member_count = lax.axis_size("seq")
    own_index = lax.axis_index("seq")
    local_heads = HEADS // member_count
    own_width = local_heads * HEAD
    offset = own_index * own_width
    text_length = text_input.shape[1]
    image_rows_dev = image_input.shape[1]
    weights = lax.all_gather(w_qkv, "fsdp", axis=0, tiled=True)
    image_triple = jnp.einsum(
        "btd,dch->btch", image_input, weights, preferred_element_type=jnp.float32
    ).astype(jnp.bfloat16)
    stacked = jnp.concatenate([image_triple, image_cotangent[:, :, None, :]], axis=2)
    arrived = lax.all_to_all(stacked, "seq", split_axis=3, concat_axis=1, tiled=True)
    own_weights = lax.dynamic_slice_in_dim(weights, offset, own_width, 2)
    text_triple = jnp.einsum(
        "btd,dch->btch", text_input, own_weights, preferred_element_type=jnp.float32
    ).astype(jnp.bfloat16)
    text_incoming = lax.dynamic_slice_in_dim(text_cotangent, offset, own_width, 2)
    joined_triple = jnp.concatenate([text_triple, arrived[:, :, :3]], axis=1)
    joined_incoming = jnp.concatenate([text_incoming, arrived[:, :, 3]], axis=1)
    batch_rows = joined_triple.shape[0]
    length = joined_triple.shape[1]
    split_triple = joined_triple.reshape(batch_rows, length, 3, local_heads, HEAD)
    split_incoming = joined_incoming.reshape(batch_rows, length, local_heads, HEAD)
    per_head = jax.vmap(head_backward, in_axes=(1, 1, 1, 1, None, None), out_axes=(2, 0))
    per_batch = jax.vmap(per_head, in_axes=(0, 0, 0, 0, None, None), out_axes=(0, 0))
    head_grads, gain_parts = per_batch(
        split_triple[:, :, 0],
        split_triple[:, :, 1],
        split_triple[:, :, 2],
        split_incoming,
        query_gain,
        key_gain,
    )
    head_grads = head_grads.reshape(batch_rows, length, 3, own_width)
    text_grads = head_grads[:, :text_length]
    image_grads = head_grads[:, text_length:]
    gain_total = lax.psum(jnp.sum(gain_parts, axis=(0, 1)), ("fsdp", "seq"))
    image_tokens = lax.all_to_all(image_grads, "seq", split_axis=1, concat_axis=3, tiled=True)
    text_partial = jnp.einsum(
        "btch,dch->btd", text_grads, own_weights, preferred_element_type=jnp.float32
    )
    text_out = lax.psum(text_partial.astype(jnp.bfloat16), "seq")
    image_out = jnp.einsum(
        "btch,dch->btd", image_tokens, weights, preferred_element_type=jnp.float32
    ).astype(jnp.bfloat16)
    text_part = jnp.einsum(
        "btd,btch->dch", text_input, text_grads, preferred_element_type=jnp.float32
    )
    whole_image = lax.all_gather(image_input, "seq", axis=1, tiled=True)

    def add_block(block, running):
        start = (block * image_rows_dev).astype(jnp.int32)
        image_block = lax.dynamic_slice_in_dim(whole_image, start, image_rows_dev, 1)
        grad_block = lax.dynamic_slice_in_dim(image_grads, start, image_rows_dev, 1)
        selected = (block == own_index).astype(jnp.float32)
        term = (
            jnp.einsum("btd,btch->dch", image_block, grad_block, preferred_element_type=jnp.float32)
            + text_part * selected
        )
        rounded = lax.optimization_barrier(term.astype(jnp.bfloat16))
        return running + rounded.astype(jnp.float32)

    start_total = jnp.zeros((image_input.shape[2], 3, own_width), jnp.float32)
    head_total = lax.fori_loop(0, member_count, add_block, start_total)
    grad_weights = lax.psum_scatter(
        head_total.astype(jnp.bfloat16), "fsdp", scatter_dimension=0, tiled=True
    ).astype(jnp.float32)
    return (image_out, text_out, grad_weights, gain_total)


def solution(mesh):
    return jax.shard_map(
        local,
        mesh=mesh,
        in_specs=(
            P("fsdp", "seq", None),
            P("fsdp", None, None),
            P("fsdp", None, None),
            P(),
            P(),
            P("fsdp", "seq", None),
            P("fsdp", None, None),
        ),
        out_specs=(P("fsdp", "seq", None), P("fsdp", None, None), P("fsdp", None, "seq"), P()),
        check_vma=False,
    )
```

profile of v0, /device:TPU:0, one launch (start us, length us, event | category | flops | bytes accessed | tf_op | source)
XLA Modules:
  0.0 548.0 jit_solution(7560957821269184910)
XLA Ops:
  8.1 6.7 %copy.122 = bf16[384,3,2048]{0,2,1:T(8,128)(2,1)} copy(bf16[384,3,2048]{2,0,1:T(8,128)(2,1)} %param.13) | data formatting | bytes 9437184 | tf_op args[2]
  14.8 178.5 %all-gather.3.cloned.1.call-done = bf16[1536,3,2048]{0,2,1:T(8,128)(2,1)} async-done(((bf16[384,3,2048]{0,2,1:T(8,128)(2,1)}), bf16[1536,3,2048]{0,2,1:T(8,128)(2,1)}) %all-gather.3.cloned.1.call-update) | async-done | bytes 18874384 | tf_op jit(solution)/shard_map/all_gather | solution.py:78
  193.3 13.7 %fusion.44 = bf16[1,128,3,2048]{3,1,2,0:T(8,128)(2,1)} fusion(bf16[1536,3,2048]{0,2,1:T(8,128)(2,1)} %all-gather.3.cloned.1.call-done, bf16[1,128,1536]{2,1,0:T(8,128)(2,1)S(1)} %copy-done.16), kind=kOutput, calls=%fused_computation.46 | convolution fusion | flops 2416705536 | bytes 20840448 | tf_op jit(solution)/shard_map/btd,dch->btch/dot_general | solution.py:79
  207.0 1.6 pad_maximum_fusion
  208.6 2.6 copy.124
  211.2 4.6 all-to-all-start
  215.9 2.0 copy.144
  218.3 2.4 fusion.80
  220.7 69.4 %all-to-all-done = bf16[1,128,4,2048]{1,2,0,3:T(4,128)(2,1)S(1)} async-done(((bf16[1,128,4,2048]{1,2,0,3:T(4,128)(2,1)}), bf16[1,128,4,2048]{1,2,0,3:T(4,128)(2,1)S(1)}, u32[]{:S(2)}, u32[]{:S(2)}) %all-to-all-start) | async-done | bytes 2097184 | tf_op jit(solution)/shard_map/all_to_all | solution.py:83
  290.1 1.7 copy.125
  291.8 2.9 copy.126
  296.0 1.7 copy.127
  302.9 52.1 %while.29 = (s32[]{:T(128)}, f32[1,2,1152,128]{3,2,1,0:T(8,128)}, f32[1,2,1152,128]{3,2,1,0:T(8,128)}, f32[4,1,2,288,128]{4,3,0,2,1:T(8,128)}, bf16[4,1,2,288,12...) while((s32[]{:T(128)}, f32[1,2,1152,128]{3,2,1,0:T(8,128)}, ...), condition=%wide.region_6.7_spmd.clone, body=%wide.region_2.6_spmd.clone.sunk | while | flops 858858048 | bytes 69760840 | solution.py:56
  302.9 2.3 fusion.129
  305.1 2.4 multiply_reduce_fusion.2
  307.5 2.2 multiply_convert_fusion.2
  309.8 2.2 fusion.130
  312.1 2.5 fusion.131
  315.9 2.3 fusion.129
  318.1 2.4 multiply_reduce_fusion.2
  320.5 2.2 multiply_convert_fusion.2
  322.8 2.2 fusion.130
  325.1 2.5 fusion.131
  328.9 2.2 fusion.129
  331.2 2.4 multiply_reduce_fusion.2
  333.6 2.2 multiply_convert_fusion.2
  335.8 2.2 fusion.130
  338.1 2.5 fusion.131
  341.9 2.3 fusion.129
  344.2 2.4 multiply_reduce_fusion.2
  346.6 2.2 multiply_convert_fusion.2
  348.9 2.2 fusion.130
  351.2 2.5 fusion.131
  355.0 2.4 copy.138
  357.8 1.7 copy.136
  364.4 2.9 convolution_bitcast_fusion.1
  367.3 6.0 %copy.146 = f32[1536,3,256]{2,0,1:T(8,128)} copy(f32[1536,3,256]{0,2,1:T(8,128)} %convolution_bitcast_fusion.1) | data formatting | bytes 9437184
  373.4 64.9 %while.30 = (s32[]{:T(128)}, f32[1536,3,256]{2,0,1:T(8,128)}, bf16[1,1024,1536]{1,2,0:T(8,128)(2,1)}, bf16[1,1024,3,256]{1,3,2,0:T(8,128)(2,1)}, s32[]{:T(128)},...) while((s32[]{:T(128)}, f32[1536,3,256]{2,0,1:T(8,128)}, ...), condition=%wide.region_11.12_spmd.clone, body=%wide.region_10.11_spmd.clone.sunk | while | flops 309067776 | bytes 19465908 | solution.py:135
  373.4 3.4 add_convert_fusion.2
  376.7 2.7 select_add_fusion.2
  379.4 3.4 add_convert_fusion.2
  382.8 5.0 select_add_fusion.2
  387.8 3.4 add_convert_fusion.2
  391.2 5.0 select_add_fusion.2
  396.3 3.4 add_convert_fusion.2
  399.6 5.0 select_add_fusion.2
  404.7 3.4 add_convert_fusion.2
  408.0 5.0 select_add_fusion.2
  413.1 3.4 add_convert_fusion.2
  416.4 5.0 select_add_fusion.2
  421.5 3.4 add_convert_fusion.2
  424.8 5.0 select_add_fusion.2
  429.9 3.4 add_convert_fusion.2
  433.3 5.0 select_add_fusion.2
  438.3 4.0 convert_element_type.125
  443.7 2.5 copy.140
  446.3 3.6 all-to-all-start.1
  449.9 3.0 fusion.47
  453.0 68.9 %psum.15 = f32[2,128]{1,0:T(2,128)} all-reduce(f32[2,128]{1,0:T(2,128)S(1)} %maximum_reduce_fusion), channel_id=1, replica_groups=mesh['fsdp'=4,'seq'=8] {'fsdp','seq'}, use_global_device_ids=true, to_apply=%region_16.17 | all-reduce | flops 256 | bytes 2048 | tf_op jit(solution)/shard_map/psum | solution.py:108
  521.9 2.3 copy.170
  524.2 2.6 reshape.317
  526.9 9.8 %fusion.48 = bf16[1,128,1536]{2,1,0:T(8,128)(2,1)} fusion(bf16[128,3,2048]{2,0,1:T(8,128)(2,1)S(1)} %reshape.317, bf16[1536,3,2048]{0,2,1:T(8,128)(2,1)} %all-gather.3.cloned.1.call-done), kind=kOutput, calls=%fused_computation.54 | convolution fusion | flops 2416115712 | bytes 20840448 | tf_op jit(solution)/shard_map/btch,dch->btd/dot_general | solution.py:114
  536.6 2.2 convert_element_type.126
  538.8 1.8 copy.191
  (132 shorter events, 18.6 us)
Async XLA Ops:
  8.0 210.1 %copy-start = (bf16[1,128,2048]{2,1,0:T(8,128)(2,1)S(1)}, bf16[1,128,2048]{2,1,0:T(8,128)(2,1)}, u32[]{:S(2)}) copy-start(bf16[1,128,2048]{2,1,0:T(8,128)(2,1)} %param.17) | copy-start | bytes 1572868
  8.0 185.3 %all-gather.3.cloned.1.call-start = ((), (), s32[]{:S(2)}) async-start(), calls=%async_computation.3 | async-start | bytes 23592960 | tf_op jit(solution)/shard_map/all_gather | solution.py:78
  14.7 178.6 %copy-start.16 = (bf16[1,128,1536]{2,1,0:T(8,128)(2,1)S(1)}, bf16[1,128,1536]{2,1,0:T(8,128)(2,1)}, u32[]{:S(2)}) copy-start(bf16[1,128,1536]{2,1,0:T(8,128)(2,1)} %param.11) | copy-start | bytes 1179652
  14.8 192.3 %copy-start.20 = (bf16[1,128,2048]{2,1,0:T(8,128)(2,1)S(1)}, bf16[1,128,2048]{2,1,0:T(8,128)(2,1)}, u32[]{:S(2)}) copy-start(bf16[1,128,2048]{2,1,0:T(8,128)(2,1)} %param.16) | copy-start | bytes 1572868
  211.2 78.9 %all-to-all-start = ((bf16[1,128,4,2048]{1,2,0,3:T(4,128)(2,1)}), bf16[1,128,4,2048]{1,2,0,3:T(4,128)(2,1)S(1)}, u32[]{:S(2)}, u32[]{:S(2)}) async-start(bf16[1,128,4,2048]{1,2,0,3:T(4,128)(2,1)} %copy.124), calls=%async_computation | async-start | bytes 4194304 | tf_op jit(solution)/shard_map/all_to_all | solution.py:83
  215.8 2.5 copy-start.14
  215.8 157.6 %all-gather.5.cloned.1.call-start = ((), (), s32[]{:S(2)}) async-start(), calls=%async_computation.5 | async-start | bytes 3538944 | tf_op jit(solution)/shard_map/all_gather | solution.py:120
  217.9 318.8 %reduce-scatter.2.cloned.1.call-start = ((), (), s32[]{:S(2)}) async-start(), calls=%async_computation.6 | async-start | bytes 2949120 | tf_op jit(solution)/shard_map/reduce_scatter | solution.py:136
  298.0 1.3 copy-start.8
  298.0 1.3 copy-start.10
  298.1 0.9 copy-start.21
  298.1 0.9 copy-start.22
  305.1 2.4 copy-start.2
  307.5 2.3 copy-start.4
  309.8 2.3 copy-start.3
  309.8 2.3 copy-start.17
  312.0 2.6 copy-start.5
  312.1 2.6 copy-start.19
  314.6 1.2 copy-start.18
  318.1 2.4 copy-start.2
  320.5 2.3 copy-start.4
  322.8 2.3 copy-start.3
  322.8 2.3 copy-start.17
  325.1 2.6 copy-start.5
  325.1 2.6 copy-start.19
  327.7 1.2 copy-start.18
  331.2 2.4 copy-start.2
  333.5 2.3 copy-start.4
  335.8 2.3 copy-start.3
  335.8 2.3 copy-start.17
  338.1 2.6 copy-start.5
  338.1 2.6 copy-start.19
  340.7 1.2 copy-start.18
  344.2 2.4 copy-start.2
  346.6 2.3 copy-start.4
  348.8 2.3 copy-start.3
  348.9 2.3 copy-start.17
  351.1 2.6 copy-start.5
  351.2 2.6 copy-start.19
  353.7 1.3 copy-start.18
  355.0 2.4 copy-start.6
  357.8 1.7 copy-start.11
  359.5 1.1 copy-start.9
  361.4 1.1 copy-start.13
  362.7 1.8 copy-start.12
  362.7 1.8 copy-start.15
  442.3 1.4 copy-start.7
  446.3 75.7 %all-to-all-start.1 = ((bf16[1,1024,3,256]{3,2,0,1:T(4,128)(2,1)}), bf16[1,1024,3,256]{3,2,0,1:T(4,128)(2,1)S(1)}, u32[]{:S(2)}, u32[]{:S(2)}) async-start(bf16[1,1024,3,256]{3,2,0,1:T(4,128)(2,1)} %copy.140), calls=%async_computation.1 | async-start | bytes 4194304 | tf_op jit(solution)/shard_map/all_to_all | solution.py:109
  449.9 88.9 %all-reduce.2.cloned.1.call-start = ((), (), s32[]{:S(2)}) async-start(), calls=%async_computation.4 | async-start | bytes 786432 | tf_op jit(solution)/shard_map/psum | solution.py:113
  526.8 13.7 %copy-start.1 = (bf16[1,128,2048]{2,1,0:T(8,128)(2,1)S(1)}, bf16[1,128,2048]{2,1,0:T(8,128)(2,1)}, u32[]{:S(2)}) copy-start(bf16[1,128,2048]{2,1,0:T(8,128)(2,1)} %param.17) | copy-start | bytes 1572868
Sparse Core Ops, SparseCore 0:
  14.9 178.3 all-gather.2
  442.5 35.8 reduce-scatter.1
Sparse Core Ops, SparseCore 1:
  218.5 70.8 all-gather.4
  453.3 69.3 all-reduce.1
where the time goes:
time: 550 us; the launch traced here: 548 us
  waiting for transfers between devices  248 us (45%)
  matrix products  101 us (18%)
  blocking collectives  68.9 us (13%)
  other arithmetic  58.1 us (11%)
  local copies, waits for them, and re-layouts  46.7 us (8%)
  between operations  15.8 us (3%)
  starting transfers between devices  8.54 us (2%)
    all_gather x1, waiting for transfers between devices, local(): weights = lax.all_gather(w_qkv, 'fsdp', axis=0, tiled=True)  179 us
    all_to_all x1, waiting for transfers between devices, local(): lax.all_to_all(stacked, 'seq', split_axis=3, concat_axis=1, tiled=True)  69.4 us
    psum x1, blocking collectives, local(): gain_total = lax.psum(jnp.sum(gain_parts, axis=(0, 1)), ('fsdp', 'seq'))  68.9 us
    add x8, other arithmetic, add_block(): return running + rounded.astype(jnp.float32)  37.9 us
    dot_general x8, matrix products, add_block(): jnp.einsum('btd,btch->dch', image_block, grad_block, preferred_element_ty...  26.9 us
    unnamed x37, local copies, waits for them, and re-layouts  20.7 us
    dot_general x1, matrix products, local(): jnp.einsum('btd,dch->btch', image_input, weights, preferred_element_type=...  13.7 us
  transfers between devices with their start and end apart: 6, of which 2 were waited for; matrix products, arithmetic and copies ran while one was open for 20% of the time, Pallas kernels for 0%

commit v1 on v0

--- a/solution.py
+++ b/solution.py
@@ -105,7 +105,9 @@
     head_grads = head_grads.reshape(batch_rows, length, 3, own_width)
     text_grads = head_grads[:, :text_length]
     image_grads = head_grads[:, text_length:]
-    gain_total = lax.psum(jnp.sum(gain_parts, axis=(0, 1)), ("fsdp", "seq"))
+    gain_total = jnp.sum(gain_parts, axis=(0, 1))
+    for p in ("seq", "fsdp"):
+        gain_total = jax.lax.psum(gain_total, p)
     image_tokens = lax.all_to_all(image_grads, "seq", split_axis=1, concat_axis=3, tiled=True)
     text_partial = jnp.einsum(
         "btch,dch->btd", text_grads, own_weights, preferred_element_type=jnp.float32

time: 550 us -> 544 us (0.989); the launches traced: 548 us -> 536 us
  blocking collectives: 68.9 us -> 56.4 us
    psum x1 -> x2, blocking collectives: 68.9 us -> 56.4 us  [local(): gain_total = jax.lax.psum(gain_total, p)]
where the time goes in v1:
time: 544 us; the launch traced here: 536 us
  waiting for transfers between devices  248 us (46%)
  matrix products  101 us (19%)
  other arithmetic  58.1 us (11%)
  blocking collectives  56.4 us (10%)
  local copies, waits for them, and re-layouts  46.7 us (9%)
  between operations  15.8 us (3%)
  starting transfers between devices  8.54 us (2%)
    all_gather x1, waiting for transfers between devices, local(): weights = lax.all_gather(w_qkv, 'fsdp', axis=0, tiled=True)  179 us
    all_to_all x1, waiting for transfers between devices, local(): lax.all_to_all(stacked, 'seq', split_axis=3, concat_axis=1, tiled=True)  69.4 us
    psum x2, blocking collectives, local(): gain_total = jax.lax.psum(gain_total, p)  56.4 us
    add x8, other arithmetic, add_block(): return running + rounded.astype(jnp.float32)  37.9 us
    dot_general x8, matrix products, add_block(): jnp.einsum('btd,btch->dch', image_block, grad_block, preferred_element_ty...  26.9 us
    unnamed x37, local copies, waits for them, and re-layouts  20.7 us
    dot_general x1, matrix products, local(): jnp.einsum('btd,dch->btch', image_input, weights, preferred_element_type=...  13.7 us
  transfers between devices with their start and end apart: 6, of which 2 were waited for; matrix products, arithmetic and copies ran while one was open for 20% of the time, Pallas kernels for 0%

profile of v1, /device:TPU:0, one launch (start us, length us, event | category | flops | bytes accessed | tf_op | source)
XLA Modules:
  0.0 535.5 jit_solution(6335178724556667758)
XLA Ops:
  8.1 6.7 %copy.122 = bf16[384,3,2048]{0,2,1:T(8,128)(2,1)} copy(bf16[384,3,2048]{2,0,1:T(8,128)(2,1)} %param.13) | data formatting | bytes 9437184 | tf_op args[2]
  14.8 178.5 %all-gather.3.cloned.1.call-done = bf16[1536,3,2048]{0,2,1:T(8,128)(2,1)} async-done(((bf16[384,3,2048]{0,2,1:T(8,128)(2,1)}), bf16[1536,3,2048]{0,2,1:T(8,128)(2,1)}) %all-gather.3.cloned.1.call-update) | async-done | bytes 18874384 | tf_op jit(solution)/shard_map/all_gather | solution.py:78
  193.3 13.7 %fusion.44 = bf16[1,128,3,2048]{3,1,2,0:T(8,128)(2,1)} fusion(bf16[1536,3,2048]{0,2,1:T(8,128)(2,1)} %all-gather.3.cloned.1.call-done, bf16[1,128,1536]{2,1,0:T(8,128)(2,1)S(1)} %copy-done.16), kind=kOutput, calls=%fused_computation.46 | convolution fusion | flops 2416705536 | bytes 20840448 | tf_op jit(solution)/shard_map/btd,dch->btch/dot_general | solution.py:79
  208.6 2.6 copy.124
  211.2 4.6 all-to-all-start
  215.9 2.0 copy.144
  218.3 2.4 fusion.80
  220.8 69.4 %all-to-all-done = bf16[1,128,4,2048]{1,2,0,3:T(4,128)(2,1)S(1)} async-done(((bf16[1,128,4,2048]{1,2,0,3:T(4,128)(2,1)}), bf16[1,128,4,2048]{1,2,0,3:T(4,128)(2,1)S(1)}, u32[]{:S(2)}, u32[]{:S(2)}) %all-to-all-start) | async-done | bytes 2097184 | tf_op jit(solution)/shard_map/all_to_all | solution.py:83
  290.1 1.7 copy.125
  291.8 2.9 copy.126
  296.0 1.7 copy.127
  302.9 52.1 %while.29 = (s32[]{:T(128)}, f32[1,2,1152,128]{3,2,1,0:T(8,128)}, f32[1,2,1152,128]{3,2,1,0:T(8,128)}, f32[4,1,2,288,128]{4,3,0,2,1:T(8,128)}, bf16[4,1,2,288,12...) while((s32[]{:T(128)}, f32[1,2,1152,128]{3,2,1,0:T(8,128)}, ...), condition=%wide.region_6.7_spmd.clone, body=%wide.region_2.6_spmd.clone.sunk | while | flops 858858048 | bytes 69760840 | solution.py:56
  302.9 2.2 fusion.129
  305.1 2.4 multiply_reduce_fusion.2
  307.5 2.2 multiply_convert_fusion.2
  309.8 2.2 fusion.130
  312.1 2.5 fusion.131
  315.9 2.3 fusion.129
  318.1 2.4 multiply_reduce_fusion.2
  320.5 2.2 multiply_convert_fusion.2
  322.8 2.2 fusion.130
  325.1 2.5 fusion.131
  328.9 2.2 fusion.129
  331.2 2.4 multiply_reduce_fusion.2
  333.6 2.2 multiply_convert_fusion.2
  335.8 2.2 fusion.130
  338.1 2.5 fusion.131
  342.0 2.3 fusion.129
  344.2 2.4 multiply_reduce_fusion.2
  346.6 2.2 multiply_convert_fusion.2
  348.9 2.2 fusion.130
  351.2 2.5 fusion.131
  355.0 2.4 copy.138
  357.8 1.7 copy.136
  364.5 2.9 convolution_bitcast_fusion.1
  367.4 6.0 %copy.146 = f32[1536,3,256]{2,0,1:T(8,128)} copy(f32[1536,3,256]{0,2,1:T(8,128)} %convolution_bitcast_fusion.1) | data formatting | bytes 9437184
  373.4 64.8 %while.30 = (s32[]{:T(128)}, f32[1536,3,256]{2,0,1:T(8,128)}, bf16[1,1024,1536]{1,2,0:T(8,128)(2,1)}, bf16[1,1024,3,256]{1,3,2,0:T(8,128)(2,1)}, s32[]{:T(128)},...) while((s32[]{:T(128)}, f32[1536,3,256]{2,0,1:T(8,128)}, ...), condition=%wide.region_11.12_spmd.clone, body=%wide.region_10.11_spmd.clone.sunk | while | flops 309067776 | bytes 19465908 | solution.py:137
  373.4 3.4 add_convert_fusion.2
  376.8 2.7 select_add_fusion.2
  379.5 3.4 add_convert_fusion.2
  382.8 5.0 select_add_fusion.2
  387.9 3.4 add_convert_fusion.2
  391.2 5.0 select_add_fusion.2
  396.3 3.4 add_convert_fusion.2
  399.6 5.0 select_add_fusion.2
  404.7 3.4 add_convert_fusion.2
  408.0 5.0 select_add_fusion.2
  413.1 3.4 add_convert_fusion.2
  416.4 5.0 select_add_fusion.2
  421.5 3.4 add_convert_fusion.2
  424.8 5.0 select_add_fusion.2
  429.8 3.4 add_convert_fusion.2
  433.2 5.0 select_add_fusion.2
  438.2 4.0 convert_element_type.125
  443.7 2.6 copy.140
  446.2 3.6 all-to-all-start.1
  449.9 3.0 fusion.47
  453.0 47.0 %psum.22 = f32[2,128]{1,0:T(2,128)S(1)} all-reduce(f32[2,128]{1,0:T(2,128)S(1)} %maximum_reduce_fusion), channel_id=1, replica_groups=mesh['fsdp'=4,'seq'=8] {'seq'}, use_global_device_ids=true, to_apply=%region_16.17 | all-reduce | flops 256 | bytes 2048 | tf_op jit(solution)/shard_map/psum | solution.py:110
  500.0 9.5 %psum.23 = f32[2,128]{1,0:T(2,128)} all-reduce(f32[2,128]{1,0:T(2,128)S(1)} %psum.22), channel_id=1, replica_groups=mesh['fsdp'=4,'seq'=8] {'fsdp'}, use_global_device_ids=true, to_apply=%region_17.18 | all-reduce | flops 256 | bytes 2048 | tf_op jit(solution)/shard_map/psum | solution.py:110
  509.4 2.3 copy.170
  511.7 2.6 reshape.317
  514.4 9.8 %fusion.48 = bf16[1,128,1536]{2,1,0:T(8,128)(2,1)} fusion(bf16[128,3,2048]{2,0,1:T(8,128)(2,1)S(1)} %reshape.317, bf16[1536,3,2048]{0,2,1:T(8,128)(2,1)} %all-gather.3.cloned.1.call-done), kind=kOutput, calls=%fused_computation.54 | convolution fusion | flops 2416115712 | bytes 20840448 | tf_op jit(solution)/shard_map/btch,dch->btd/dot_general | solution.py:116
  524.2 2.2 convert_element_type.126
  526.3 1.8 copy.191
  (133 shorter events, 20.2 us)
Async XLA Ops:
  8.0 210.1 %copy-start = (bf16[1,128,2048]{2,1,0:T(8,128)(2,1)S(1)}, bf16[1,128,2048]{2,1,0:T(8,128)(2,1)}, u32[]{:S(2)}) copy-start(bf16[1,128,2048]{2,1,0:T(8,128)(2,1)} %param.17) | copy-start | bytes 1572868
  8.0 185.3 %all-gather.3.cloned.1.call-start = ((), (), s32[]{:S(2)}) async-start(), calls=%async_computation.3 | async-start | bytes 23592960 | tf_op jit(solution)/shard_map/all_gather | solution.py:78
  14.7 178.6 %copy-start.16 = (bf16[1,128,1536]{2,1,0:T(8,128)(2,1)S(1)}, bf16[1,128,1536]{2,1,0:T(8,128)(2,1)}, u32[]{:S(2)}) copy-start(bf16[1,128,1536]{2,1,0:T(8,128)(2,1)} %param.11) | copy-start | bytes 1179652
  14.8 192.3 %copy-start.20 = (bf16[1,128,2048]{2,1,0:T(8,128)(2,1)S(1)}, bf16[1,128,2048]{2,1,0:T(8,128)(2,1)}, u32[]{:S(2)}) copy-start(bf16[1,128,2048]{2,1,0:T(8,128)(2,1)} %param.16) | copy-start | bytes 1572868
  211.2 78.9 %all-to-all-start = ((bf16[1,128,4,2048]{1,2,0,3:T(4,128)(2,1)}), bf16[1,128,4,2048]{1,2,0,3:T(4,128)(2,1)S(1)}, u32[]{:S(2)}, u32[]{:S(2)}) async-start(bf16[1,128,4,2048]{1,2,0,3:T(4,128)(2,1)} %copy.124), calls=%async_computation | async-start | bytes 4194304 | tf_op jit(solution)/shard_map/all_to_all | solution.py:83
  215.8 2.5 copy-start.14
  215.8 157.6 %all-gather.5.cloned.1.call-start = ((), (), s32[]{:S(2)}) async-start(), calls=%async_computation.5 | async-start | bytes 3538944 | tf_op jit(solution)/shard_map/all_gather | solution.py:122
  217.9 306.3 %reduce-scatter.2.cloned.1.call-start = ((), (), s32[]{:S(2)}) async-start(), calls=%async_computation.6 | async-start | bytes 2949120 | tf_op jit(solution)/shard_map/reduce_scatter | solution.py:138
  298.0 1.3 copy-start.8
  298.1 1.3 copy-start.10
  298.1 0.9 copy-start.21
  298.1 0.9 copy-start.22
  305.1 2.4 copy-start.2
  307.5 2.3 copy-start.4
  309.8 2.3 copy-start.3
  309.8 2.3 copy-start.17
  312.0 2.6 copy-start.5
  312.1 2.6 copy-start.19
  314.6 1.2 copy-start.18
  318.1 2.4 copy-start.2
  320.5 2.3 copy-start.4
  322.8 2.3 copy-start.3
  322.8 2.3 copy-start.17
  325.1 2.6 copy-start.5
  325.1 2.6 copy-start.19
  327.7 1.3 copy-start.18
  331.2 2.4 copy-start.2
  333.5 2.3 copy-start.4
  335.8 2.3 copy-start.3
  335.8 2.3 copy-start.17
  338.1 2.6 copy-start.5
  338.1 2.6 copy-start.19
  340.7 1.3 copy-start.18
  344.2 2.4 copy-start.2
  346.6 2.3 copy-start.4
  348.9 2.3 copy-start.3
  348.9 2.3 copy-start.17
  351.1 2.6 copy-start.5
  351.2 2.6 copy-start.19
  353.7 1.3 copy-start.18
  355.0 2.4 copy-start.6
  357.8 1.7 copy-start.11
  359.5 1.1 copy-start.9
  361.4 1.1 copy-start.13
  362.7 1.8 copy-start.12
  362.7 1.8 copy-start.15
  442.3 1.4 copy-start.7
  446.2 63.2 %all-to-all-start.1 = ((bf16[1,1024,3,256]{3,2,0,1:T(4,128)(2,1)}), bf16[1,1024,3,256]{3,2,0,1:T(4,128)(2,1)S(1)}, u32[]{:S(2)}, u32[]{:S(2)}) async-start(bf16[1,1024,3,256]{3,2,0,1:T(4,128)(2,1)} %copy.140), calls=%async_computation.1 | async-start | bytes 4194304 | tf_op jit(solution)/shard_map/all_to_all | solution.py:111
  449.9 76.5 %all-reduce.2.cloned.1.call-start = ((), (), s32[]{:S(2)}) async-start(), calls=%async_computation.4 | async-start | bytes 786432 | tf_op jit(solution)/shard_map/psum | solution.py:115
  514.3 13.8 %copy-start.1 = (bf16[1,128,2048]{2,1,0:T(8,128)(2,1)S(1)}, bf16[1,128,2048]{2,1,0:T(8,128)(2,1)}, u32[]{:S(2)}) copy-start(bf16[1,128,2048]{2,1,0:T(8,128)(2,1)} %param.17) | copy-start | bytes 1572868
Sparse Core Ops, SparseCore 0:
  14.9 178.3 all-gather.2
  442.4 35.3 reduce-scatter.1
Sparse Core Ops, SparseCore 1:
  218.5 70.8 all-gather.4
  453.2 67.3 all-reduce.1
